TPU v7x, 256 devices: a whole 4x4x8 slice. The times are simulated.
256 devices in a mesh: dp: 32 (over z, x_hi, core), mp: 8 (over x_lo, y).
Axes of the slice: x: 4 (x_hi: 2, x_lo: 2; x = x_hi * 2 + x_lo), y: 4, z: 8, core: 2. Of those that a mesh axis runs over, the one named last changes fastest.
Arguments:
- tokens: bfloat16 [1024, 16384], P('dp', 'mp'), may hold values from -6 to 6
- gate_weight: bfloat16 [16384, 28672], P('mp', 'dp'), may hold values from -0.046875 to 0.046875
- up_weight: bfloat16 [16384, 28672], P('mp', 'dp'), may hold values from -0.046875 to 0.046875
- down_weight: bfloat16 [28672, 16384], P('dp', 'mp'), may hold values from -0.03125 to 0.03125
Outputs:
- mixed: bfloat16 [1024, 16384], P('dp', 'mp')
All inputs are finite; a program needn't handle non-finite values.
Results may differ from a plain program's by a relative error of at most 0.0049.
Values may be sent and summed in bfloat16 or wider, within the bound.
A program may use at most 64 MiB of HBM per device.

v0:
```python
import jax
import jax.numpy as jnp
from jax import lax
from jax.sharding import PartitionSpec as P


def in_order(blocks, dim):
    blocks = jnp.moveaxis(blocks, 0, dim)
    shape = blocks.shape
    return blocks.reshape(*shape[:dim], shape[dim] * shape[dim + 1], *shape[dim + 2 :])


def sent_to_all(x, axis):
    copies = jnp.broadcast_to(x, (lax.axis_size(axis), *x.shape))
    return lax.all_to_all(copies, axis, split_axis=0, concat_axis=0, tiled=True)


def collect(x, axis, dim):
    return in_order(sent_to_all(x, axis), dim)


def per_device(tokens, gate_weight, up_weight, down_weight):
    width = gate_weight.shape[1]
    piece = lax.all_gather(tokens, "dp", axis=0, tiled=True)
    gate_part = jnp.dot(piece, gate_weight, preferred_element_type=jnp.float32)
    up_part = jnp.dot(piece, up_weight, preferred_element_type=jnp.float32)
    partial_both = jnp.concatenate([gate_part, up_part], axis=1)
    share = lax.psum_scatter(partial_both, "mp", scatter_dimension=0, tiled=True)
    own_rows = (jax.nn.silu(share[:, :width]) * share[:, width:]).astype(jnp.bfloat16)
    hidden = collect(own_rows, "mp", 0)
    mixed = lax.psum_scatter(
        jnp.dot(hidden, down_weight, preferred_element_type=jnp.float32),
        "dp",
        scatter_dimension=0,
        tiled=True,
    )
    return mixed.astype(jnp.bfloat16)


def solution(mesh):
    return jax.shard_map(
        per_device,
        mesh=mesh,
        in_specs=(P("dp", "mp"), P("mp", "dp"), P("mp", "dp"), P("dp", "mp")),
        out_specs=P("dp", "mp"),
        check_vma=False,
    )
```

profile of v0, /device:TPU:8, one launch (start us, length us, event | category | flops | bytes accessed | tf_op | source)
XLA Modules:
  0.0 394.5 jit_solution(867062498399786874)
XLA Ops:
  6.5 0.0 all-gather.2.cloned.1.call-start
  6.5 0.7 all-gather.2.cloned.1.call-update
  7.3 0.0 reduce-scatter.3.cloned.1.call-start
  7.3 92.3 %all-gather.2.cloned.1.call-done = bf16[1024,2048]{1,0:T(8,128)(2,1)} async-done(((bf16[32,2048]{1,0:T(8,128)(2,1)}), bf16[1024,2048]{1,0:T(8,128)(2,1)}) %all-gather.2.cloned.1.call-update) | async-done | bytes 4194320 | tf_op jit(solution)/shard_map/all_gather | solution.py:24
  99.6 0.0 copy-start
  99.6 0.0 copy-start.1
  99.6 7.1 %fusion.2 = f32[1024,896]{0,1:T(8,128)S(1)} fusion(bf16[1024,2048]{1,0:T(8,128)(2,1)} %all-gather.2.cloned.1.call-done, bf16[2048,896]{1,0:T(8,128)(2,1)} %param.6), kind=kOutput, calls=%fused_computation.4 | convolution fusion | flops 3758096384 | bytes 11534336 | tf_op jit(solution)/shard_map/dot_general | solution.py:26
  106.7 0.0 copy-done
  106.7 0.0 copy-done.1
  106.7 4.2 %fusion.1 = f32[1024,896]{0,1:T(8,128)S(1)} fusion(bf16[1024,2048]{1,0:T(8,128)(2,1)S(1)} %copy-done, bf16[2048,896]{1,0:T(8,128)(2,1)S(1)} %copy-done.1), kind=kOutput, calls=%fused_computation.3 | convolution fusion | flops 3758096384 | bytes 11534336 | tf_op jit(solution)/shard_map/dot_general | solution.py:25
  111.0 3.7 pad_maximum_fusion
  114.6 0.0 reduce-scatter.3.cloned.1.call-update
  114.6 0.0 reduce-scatter.5.cloned.1.call-start
  114.7 80.1 %reduce-scatter.3.cloned.1.call-done = f32[128,1792]{0,1:T(8,128)} async-done(((f32[1024,1792]{0,1:T(8,128)}), f32[128,1792]{0,1:T(8,128)}) %reduce-scatter.3.cloned.1.call-update) | async-done | bytes 917520 | tf_op jit(solution)/shard_map/reduce_scatter | solution.py:28
  194.8 1.3 fusion
  196.1 0.2 copy.5
  196.2 0.0 copy-start.2
  196.2 0.2 broadcast_in_dim.3
  196.5 28.2 %all_to_all.5 = bf16[8,128,896]{2,1,0:T(8,128)(2,1)S(1)} all-to-all(bf16[8,128,896]{2,1,0:T(8,128)(2,1)S(1)} %broadcast_in_dim.3), channel_id=1, replica_groups=mesh['dp'=32,'mp'=8] {'mp'}, dimensions={0} | all-to-all | bytes 3670016 | tf_op jit(solution)/shard_map/all_to_all | solution.py:15
  224.6 0.0 copy-done.2
  224.6 6.8 %fusion.3 = f32[1024,2048]{1,0:T(8,128)} fusion(bf16[1024,896]{1,0:T(8,128)(2,1)S(1)} %bitcast.7, bf16[896,2048]{1,0:T(8,128)(2,1)S(1)} %copy-done.2), kind=kOutput, calls=%fused_computation.5 | convolution fusion | flops 3758096384 | bytes 13893632 | tf_op jit(solution)/shard_map/dot_general | solution.py:32
  231.4 0.0 reduce-scatter.5.cloned.1.call-update
  231.4 154.9 %reduce-scatter.5.cloned.1.call-done = f32[32,2048]{1,0:T(8,128)} async-done(((f32[1024,2048]{1,0:T(8,128)}), f32[32,2048]{1,0:T(8,128)}) %reduce-scatter.5.cloned.1.call-update) | async-done | bytes 262160 | tf_op jit(solution)/shard_map/reduce_scatter | solution.py:31
  386.3 1.6 convert_element_type.7
Async XLA Ops:
  6.5 93.1 %all-gather.2.cloned.1.call-start = ((), (), s32[]{:S(2)}) async-start(), calls=%async_computation.3 | async-start | bytes 4325376 | tf_op jit(solution)/shard_map/all_gather | solution.py:24
  7.3 187.5 %reduce-scatter.3.cloned.1.call-start = ((), (), s32[]{:S(2)}) async-start(), calls=%async_computation.4 | async-start | bytes 8257536 | tf_op jit(solution)/shard_map/reduce_scatter | solution.py:28
  99.6 7.1 %copy-start = (bf16[1024,2048]{1,0:T(8,128)(2,1)S(1)}, bf16[1024,2048]{1,0:T(8,128)(2,1)}, u32[]{:S(2)}) copy-start(bf16[1024,2048]{1,0:T(8,128)(2,1)} %all-gather.2.cloned.1.call-done) | copy-start | bytes 12582916
  99.6 7.1 %copy-start.1 = (bf16[2048,896]{1,0:T(8,128)(2,1)S(1)}, bf16[2048,896]{1,0:T(8,128)(2,1)}, u32[]{:S(2)}) copy-start(bf16[2048,896]{1,0:T(8,128)(2,1)} %param.5) | copy-start | bytes 11010052
  114.6 271.7 %reduce-scatter.5.cloned.1.call-start = ((), (), s32[]{:S(2)}) async-start(), calls=%async_computation.5 | async-start | bytes 8650752 | tf_op jit(solution)/shard_map/reduce_scatter | solution.py:31
  196.2 28.4 %copy-start.2 = (bf16[896,2048]{1,0:T(8,128)(2,1)S(1)}, bf16[896,2048]{1,0:T(8,128)(2,1)}, u32[]{:S(2)}) copy-start(bf16[896,2048]{1,0:T(8,128)(2,1)} %param.7) | copy-start | bytes 11010052
Sparse Core Ops, SparseCore 0:
  10.1 89.4 all-gather.1
  114.8 79.9 reduce-scatter.2
  231.6 154.7 reduce-scatter.4
where the time goes:
time: 395 us; the launch traced here: 394 us
  waiting for transfers between devices  328 us (83%)
  blocking collectives  28.2 us (7%)
  matrix products  18.1 us (5%)
  between operations  13.2 us (3%)
  other arithmetic  6.57 us (2%)
    reduce_scatter x1, waiting for transfers between devices, per_device(): lax.psum_scatter(jnp.dot(hidden, down_weight, preferred_element_type=jnp....  155 us
    all_gather x1, waiting for transfers between devices, per_device(): piece = lax.all_gather(tokens, 'dp', axis=0, tiled=True)  92.3 us
    reduce_scatter x1, waiting for transfers between devices, per_device(): lax.psum_scatter(partial_both, 'mp', scatter_dimension=0, tiled=True)  80.1 us
    all_to_all x1, blocking collectives, sent_to_all(): return lax.all_to_all(copies, axis, split_axis=0, concat_axis=0, tiled=True)  28.2 us
  transfers between devices with their start and end apart: 3, of which 3 were waited for; matrix products, arithmetic and copies ran while one was open for 0% of the time, Pallas kernels for 0%

commit v1 on v0

--- a/solution.py
+++ b/solution.py
@@ -21,7 +21,9 @@
 
 def per_device(tokens, gate_weight, up_weight, down_weight):
     width = gate_weight.shape[1]
-    piece = lax.all_gather(tokens, "dp", axis=0, tiled=True)
+    piece = jnp.concatenate(
+        lax.all_to_all(jnp.stack([tokens] * lax.axis_size("dp")), "dp", 0, 0), axis=0
+    )
     gate_part = jnp.dot(piece, gate_weight, preferred_element_type=jnp.float32)
     up_part = jnp.dot(piece, up_weight, preferred_element_type=jnp.float32)
     partial_both = jnp.concatenate([gate_part, up_part], axis=1)

time: 395 us -> 407 us (1.030)
  blocking collectives: 28.2 us -> 136 us
  waiting for transfers between devices: 328 us -> 235 us
    all_to_all x0 -> x1, blocking collectives: none -> 107 us  [per_device(): lax.all_to_all(jnp.stack([tokens] * lax.axis_size('dp')), 'dp', 0, 0)]
    all_gather x1 -> x0, waiting for transfers between devices: 92.3 us -> none  [per_device(): piece = lax.all_gather(tokens, 'dp', axis=0, tiled=True)]
  transfers between devices with their start and end apart: 3 -> 2, of which waited for: 3 -> 2; matrix products, arithmetic and copies ran while one was open for 0% -> 0% of each run, Pallas kernels for 0% -> 0%
where the time goes in v1:
time: 407 us
  waiting for transfers between devices  235 us (58%)
  blocking collectives  136 us (33%)
  matrix products  15.1 us (4%)
  between operations  13.5 us (3%)
  other arithmetic  6.57 us (2%)
    reduce_scatter x1, waiting for transfers between devices, per_device(): lax.psum_scatter(jnp.dot(hidden, down_weight, preferred_element_type=jnp....  155 us
    all_to_all x1, blocking collectives, per_device(): lax.all_to_all(jnp.stack([tokens] * lax.axis_size('dp')), 'dp', 0, 0)  107 us
    reduce_scatter x1, waiting for transfers between devices, per_device(): lax.psum_scatter(partial_both, 'mp', scatter_dimension=0, tiled=True)  80.2 us
    all_to_all x1, blocking collectives, sent_to_all(): return lax.all_to_all(copies, axis, split_axis=0, concat_axis=0, tiled=True)  28.2 us
  transfers between devices with their start and end apart: 2, of which 2 were waited for; matrix products, arithmetic and copies ran while one was open for 0% of the time, Pallas kernels for 0%

profile of v1, /device:TPU:8, one launch (start us, length us, event | category | flops | bytes accessed | tf_op | source)
XLA Modules:
  0.0 407.3 jit_solution(17564352064960186925)
XLA Ops:
  6.5 0.0 reduce-scatter.3.cloned.1.call-start
  6.5 1.4 stack.2
  8.0 0.0 copy-start
  8.0 107.4 %all_to_all.10 = bf16[32,32,2048]{2,1,0:T(8,128)(2,1)S(1)} all-to-all(bf16[32,32,2048]{2,1,0:T(8,128)(2,1)S(1)} %stack.2), channel_id=1, replica_groups=mesh['dp'=32,'mp'=8] {'dp'}, dimensions={0} | all-to-all | bytes 8388608 | tf_op jit(solution)/shard_map/all_to_all | solution.py:25
  115.3 0.0 copy-done
  115.3 0.0 copy-start.1
  115.3 4.2 %fusion.2 = f32[1024,896]{0,1:T(8,128)S(1)} fusion(bf16[1024,2048]{1,0:T(8,128)(2,1)S(1)} %bitcast.8, bf16[2048,896]{1,0:T(8,128)(2,1)S(1)} %copy-done), kind=kOutput, calls=%fused_computation.4 | convolution fusion | flops 3758096384 | bytes 11534336 | tf_op jit(solution)/shard_map/dot_general | solution.py:28
  119.6 0.0 copy-done.1
  119.6 4.2 %fusion.1 = f32[1024,896]{0,1:T(8,128)S(1)} fusion(bf16[1024,2048]{1,0:T(8,128)(2,1)S(1)} %bitcast.9, bf16[2048,896]{1,0:T(8,128)(2,1)S(1)} %copy-done.1), kind=kOutput, calls=%fused_computation.3 | convolution fusion | flops 3758096384 | bytes 11534336 | tf_op jit(solution)/shard_map/dot_general | solution.py:27
  123.8 3.7 pad_maximum_fusion
  127.5 0.0 reduce-scatter.3.cloned.1.call-update
  127.5 0.0 reduce-scatter.5.cloned.1.call-start
  127.6 80.2 %reduce-scatter.3.cloned.1.call-done = f32[128,1792]{0,1:T(8,128)} async-done(((f32[1024,1792]{0,1:T(8,128)}), f32[128,1792]{0,1:T(8,128)}) %reduce-scatter.3.cloned.1.call-update) | async-done | bytes 917520 | tf_op jit(solution)/shard_map/reduce_scatter | solution.py:30
  207.8 1.3 fusion
  209.1 0.2 copy.5
  209.2 0.0 copy-start.2
  209.2 0.2 broadcast_in_dim.3
  209.5 28.2 %all_to_all.11 = bf16[8,128,896]{2,1,0:T(8,128)(2,1)S(1)} all-to-all(bf16[8,128,896]{2,1,0:T(8,128)(2,1)S(1)} %broadcast_in_dim.3), channel_id=1, replica_groups=mesh['dp'=32,'mp'=8] {'mp'}, dimensions={0} | all-to-all | bytes 3670016 | tf_op jit(solution)/shard_map/all_to_all | solution.py:15
  237.6 0.0 copy-done.2
  237.6 6.6 %fusion.3 = f32[1024,2048]{1,0:T(8,128)} fusion(bf16[1024,896]{1,0:T(8,128)(2,1)S(1)} %bitcast.10, bf16[896,2048]{1,0:T(8,128)(2,1)S(1)} %copy-done.2), kind=kOutput, calls=%fused_computation.5 | convolution fusion | flops 3758096384 | bytes 13893632 | tf_op jit(solution)/shard_map/dot_general | solution.py:34
  244.3 0.0 reduce-scatter.5.cloned.1.call-update
  244.3 154.5 %reduce-scatter.5.cloned.1.call-done = f32[32,2048]{1,0:T(8,128)} async-done(((f32[1024,2048]{1,0:T(8,128)}), f32[32,2048]{1,0:T(8,128)}) %reduce-scatter.5.cloned.1.call-update) | async-done | bytes 262160 | tf_op jit(solution)/shard_map/reduce_scatter | solution.py:33
  398.8 1.6 convert_element_type.7
Async XLA Ops:
  6.5 201.2 %reduce-scatter.3.cloned.1.call-start = ((), (), s32[]{:S(2)}) async-start(), calls=%async_computation.4 | async-start | bytes 8257536 | tf_op jit(solution)/shard_map/reduce_scatter | solution.py:30
  8.0 107.4 %copy-start = (bf16[2048,896]{1,0:T(8,128)(2,1)S(1)}, bf16[2048,896]{1,0:T(8,128)(2,1)}, u32[]{:S(2)}) copy-start(bf16[2048,896]{1,0:T(8,128)(2,1)} %param.6) | copy-start | bytes 11010052
  115.3 4.2 %copy-start.1 = (bf16[2048,896]{1,0:T(8,128)(2,1)S(1)}, bf16[2048,896]{1,0:T(8,128)(2,1)}, u32[]{:S(2)}) copy-start(bf16[2048,896]{1,0:T(8,128)(2,1)} %param.5) | copy-start | bytes 11010052
  127.5 271.3 %reduce-scatter.5.cloned.1.call-start = ((), (), s32[]{:S(2)}) async-start(), calls=%async_computation.5 | async-start | bytes 8650752 | tf_op jit(solution)/shard_map/reduce_scatter | solution.py:33
  209.2 28.4 %copy-start.2 = (bf16[896,2048]{1,0:T(8,128)(2,1)S(1)}, bf16[896,2048]{1,0:T(8,128)(2,1)}, u32[]{:S(2)}) copy-start(bf16[896,2048]{1,0:T(8,128)(2,1)} %param.7) | copy-start | bytes 11010052
Sparse Core Ops, SparseCore 0:
  127.7 80.0 reduce-scatter.2
  244.4 154.3 reduce-scatter.4
